TPU v7x, 256 devices: a whole 4x4x8 slice. The times are simulated.
256 devices in a mesh: dp: 32 (over z, y_lo, core), expert: 8 (over y_hi, x).
Axes of the slice: x: 4, y: 4 (y_hi: 2, y_lo: 2; y = y_hi * 2 + y_lo), z: 8, core: 2. Of those that a mesh axis runs over, the one named last changes fastest.
Arguments:
- tokens: bfloat16 [2048, 6144], P(('dp', 'expert')), may hold values from -6 to 6
- router_now: float32 [6144, 8], P('dp'), may hold values from -0.078125 to 0.078125
- router_next: float32 [6144, 8], P('dp'), may hold values from -0.078125 to 0.078125
- w_gate: bfloat16 [8, 6144, 8192], P('expert', None, 'dp'), may hold values from -0.078125 to 0.078125
- w_up: bfloat16 [8, 6144, 8192], P('expert', None, 'dp'), may hold values from -0.078125 to 0.078125
- w_down: bfloat16 [8, 8192, 6144], P('expert', 'dp'), may hold values from -0.0625 to 0.0625
- expert_ids: int32 [2048, 2], P(('dp', 'expert')), may hold values from 0 to 7, all different within a row; in each aligned block of 8 rows (0 to 7, 8 to 15, ...) at most 4 rows name the same one
- next_ids: int32 [2048, 2], P(('dp', 'expert')), may hold values from 0 to 7, all different within a row
Outputs:
- layer_out: bfloat16 [2048, 6144], P(('dp', 'expert'))
- next_logits: float32 [2048, 8], P(('dp', 'expert'))
- next_weights: float32 [2048, 2], P(('dp', 'expert'))
Inputs may be any that keep to these rules, and one draw needn't show every extreme that they name: `expert_ids`: each row names 2 different experts. Among the 8 rows of one device no expert is named by more than 4 rows, and on some devices one expert is named by exactly 4 rows. `next_ids`: each row names 2 different experts.
All inputs are finite; a program needn't handle non-finite values.
Results may differ from a plain program's by a relative error of at most 0.013.
Values may be sent and summed in bfloat16 or wider, within the bound.
No kernel may reach another device: no remote copies, remote signals or barrier semaphores. Data moves between devices by JAX's collectives and lax.ppermute only.
A program may use at most 128 MiB of HBM per device.

v0:
```python
import jax
import jax.numpy as jnp
from jax import lax
from jax.sharding import PartitionSpec as P

CAP = 4
epsilon = 1e-05


def in_one_piece(arrays, axis, dim, along):
    both = jnp.concatenate(arrays, axis=along)
    filled, at, outs = (lax.all_gather(both, axis, axis=dim, tiled=True), 0, [])
    for a in arrays:
        outs.append(lax.slice_in_dim(filled, at, at + a.shape[along], axis=along))
        at += a.shape[along]
    return tuple(outs)


def rms_normed(values):
    return values * lax.rsqrt(jnp.mean(values * values, axis=-1, keepdims=True) + epsilon)


def pair_weights(logits, chosen):
    picked = jnp.take_along_axis(logits, chosen, axis=1)
    first = jax.nn.sigmoid(picked[:, 0] - picked[:, 1])
    return jnp.stack([first, 1.0 - first], axis=1)


def on_device(tokens, router_now, router_next, w_gate, w_up, w_down, expert_ids, next_ids):
    whole_now, whole_next = in_one_piece((router_now, router_next), "dp", 0, 1)
    resid = tokens.astype(jnp.float32)
    normed = rms_normed(resid)
    logits = jnp.dot(
        normed, whole_now, precision=lax.Precision.HIGHEST, preferred_element_type=jnp.float32
    )
    weights = pair_weights(logits, expert_ids)
    rounded = normed.astype(jnp.bfloat16)
    expert_count = whole_now.shape[1]
    per_device = w_gate.shape[0]
    groups = lax.axis_size("expert")
    tok_count = tokens.shape[0]
    top_count = expert_ids.shape[1]
    width = tokens.shape[1]
    pairs = tok_count * top_count
    chosen = expert_ids.reshape(pairs)
    onehot = (chosen[:, None] == jnp.arange(expert_count, dtype=jnp.int32)[None, :]).astype(
        jnp.int32
    )
    ranks = jnp.sum((jnp.cumsum(onehot, axis=0) - onehot) * onehot, axis=1)
    places = chosen * CAP + ranks
    place_table = (
        places[:, None] == jnp.arange(expert_count * CAP, dtype=jnp.int32)[None, :]
    ).astype(jnp.float32)
    owners = (
        (jnp.arange(pairs, dtype=jnp.int32) // top_count)[:, None]
        == jnp.arange(tok_count, dtype=jnp.int32)[None, :]
    ).astype(jnp.float32)
    sender = jnp.dot(place_table.T, owners, preferred_element_type=jnp.float32)
    dispatched = jnp.dot(
        sender.astype(jnp.bfloat16), rounded, preferred_element_type=jnp.float32
    ).astype(jnp.bfloat16)
    dispatched = dispatched.reshape(groups, per_device, CAP, width)
    received = lax.all_to_all(dispatched, "expert", split_axis=0, concat_axis=0, tiled=True)
    combine = jnp.sum(
        (place_table * weights.reshape(pairs)[:, None]).reshape(
            tok_count, top_count, expert_count * CAP
        ),
        axis=1,
    )
    hidden_list = []
    local = 0
    arriving = received[:, local].reshape(groups * CAP, width)

    def activate(piece, start, local=local):
        gate = jnp.dot(piece, w_gate[local], preferred_element_type=jnp.float32)
        upward = jnp.dot(piece, w_up[local], preferred_element_type=jnp.float32)
        return (jax.nn.silu(gate) * upward).astype(jnp.bfloat16)

    hidden_list.append(activate(lax.all_gather(arriving, "dp", axis=0, tiled=True), jnp.int32(0)))
    local = 0

    def project(start, count, local=local):
        block = hidden_list[local]
        return jnp.dot(block, w_down[local], preferred_element_type=jnp.float32)

    reduced = lax.psum_scatter(
        project(jnp.int32(0), groups * CAP * lax.axis_size("dp")).astype(jnp.bfloat16),
        "dp",
        scatter_dimension=0,
        tiled=True,
    ).astype(jnp.float32)
    returned_rows = [reduced.reshape(groups, CAP, width)]
    stacked = jnp.stack(returned_rows, axis=1)
    back = (
        lax.all_to_all(
            stacked.astype(jnp.bfloat16), "expert", split_axis=0, concat_axis=0, tiled=True
        )
        .astype(stacked.dtype)
        .reshape(expert_count * CAP, width)
    )
    mixture = jnp.dot(
        combine, back, precision=lax.Precision.HIGHEST, preferred_element_type=jnp.float32
    )
    summed = resid + mixture
    layer_out = summed.astype(jnp.bfloat16)
    next_logits = jnp.dot(
        rms_normed(summed),
        whole_next,
        precision=lax.Precision.HIGHEST,
        preferred_element_type=jnp.float32,
    )
    next_weights = pair_weights(next_logits, next_ids)
    return (layer_out, next_logits, next_weights)


def solution(mesh):
    in_specs = (
        P(("dp", "expert"), None),
        P("dp", None),
        P("dp", None),
        P("expert", None, "dp"),
        P("expert", None, "dp"),
        P("expert", "dp", None),
        P(("dp", "expert"), None),
        P(("dp", "expert"), None),
    )
    out_specs = (P(("dp", "expert"), None), P(("dp", "expert"), None), P(("dp", "expert"), None))
    return jax.shard_map(
        on_device, mesh=mesh, in_specs=in_specs, out_specs=out_specs, check_vma=False
    )
```

profile of v0, /device:TPU:2, one launch (start us, length us, event | category | flops | bytes accessed | tf_op | source)
XLA Modules:
  0.0 328.4 jit_solution(14889637307065772511)
XLA Ops:
  7.2 0.9 copy.58
  8.1 0.1 eq.48
  8.2 0.1 fusion.30
  8.3 0.2 select_reduce_fusion.1
  8.5 0.5 and_select_fusion.2
  9.0 1.1 fusion.21
  10.1 1.5 convolution_convert_fusion.1
  11.6 0.9 reshape.88
  12.4 16.5 %all_to_all.10 = bf16[8,1,4,6144]{3,2,1,0:T(4,128)(2,1)S(1)} all-to-all(bf16[8,1,4,6144]{3,2,1,0:T(4,128)(2,1)} %bitcast.34), channel_id=1, replica_groups=mesh['dp'=32,'expert'=8] {'expert'}, dimensions={0} | all-to-all | bytes 786432 | tf_op jit(solution)/shard_map/all_to_all | solution.py:63
  28.9 0.8 reshape_squeeze.3
  29.8 0.0 reduce-scatter.2.cloned.1.call-start
  29.8 79.3 %all-gather.3.cloned.1.call-done = bf16[1024,6144]{1,0:T(8,128)(2,1)} async-done(((bf16[32,6144]{1,0:T(8,128)(2,1)}), bf16[1024,6144]{1,0:T(8,128)(2,1)}) %all-gather.3.cloned.1.call-update) | async-done | bytes 12582928 | tf_op jit(solution)/shard_map/all_gather | solution.py:79
  109.1 9.9 %fusion.3 = f32[1024,256]{1,0:T(8,128)} fusion(bf16[1024,6144]{1,0:T(8,128)(2,1)} %all-gather.3.cloned.1.call-done, bf16[1,6144,256]{2,1,0:T(8,128)(2,1)} %param.13), kind=kOutput, calls=%fused_computation.8 | convolution fusion | flops 3221225472 | bytes 16777216 | tf_op jit(solution)/shard_map/dot_general | solution.py:75
  119.0 19.8 %convolution_convert_fusion = bf16[1024,6144]{1,0:T(8,128)(2,1)} fusion(bf16[1,256,6144]{2,1,0:T(8,128)(2,1)S(1)} %copy-done, bf16[1024,6144]{1,0:T(8,128)(2,1)} %all-gather.3.cloned.1.call-done, bf16[1,6144,256]{2,1,0:T(8,128)(2,1)} %param.14, f32[1024,256]{1,0:T(8,128)} %fusion.3), kind=kOutput, calls=%fused_computation.2 | convolution fusion | flops 6450315264 | bytes 32505856 | tf_op jit(solution)/shard_map/dot_general | solution.py:84
  138.9 0.1 reduce_sum.39
  139.0 0.6 multiply_add_fusion
  139.6 0.1 copy.65
  139.7 0.1 copy.66
  139.8 0.1 reshape.116
  139.9 36.9 %all-gather = f32[32,192,16]{1,2,0:T(8,128)S(1)} all-gather(f32[1,192,16]{1,2,0:T(8,128)S(1)} %maximum_bitcast_fusion), channel_id=1, replica_groups=mesh['dp'=32,'expert'=8] {'dp'}, dimensions={0}, use_global_device_ids=true | all-gather | bytes 405504 | tf_op jit(solution)/shard_map/all_gather | solution.py:12
  176.8 1.1 copy.64
  177.9 1.3 reshape.114
  179.1 1.5 fusion.20
  180.6 0.7 gather_fusion
  181.3 0.1 reshape.119
  181.4 0.8 copy.70
  182.1 0.6 clamp_shift-left_fusion
  182.7 0.1 broadcast_subtract_fusion.1
  182.8 106.2 %reduce-scatter.2.cloned.1.call-done = bf16[32,6144]{1,0:T(8,128)(2,1)} async-done(((bf16[1024,6144]{1,0:T(8,128)(2,1)}), bf16[32,6144]{1,0:T(8,128)(2,1)}) %reduce-scatter.2.cloned.1.call-update) | async-done | bytes 393232 | tf_op jit(solution)/shard_map/reduce_scatter | solution.py:86
  289.1 1.9 convert_element_type.47
  290.9 16.1 %all-to-all-start.1 = ((bf16[8,1,4,6144]{3,2,1,0:T(4,128)(2,1)}), bf16[8,1,4,6144]{3,2,1,0:T(4,128)(2,1)}, u32[]{:S(2)}, u32[]{:S(2)}) async-start(bf16[8,1,4,6144]{3,2,1,0:T(4,128)(2,1)} %bitcast.33), calls=%async_computation.2 | async-start | bytes 786432 | tf_op jit(solution)/shard_map/all_to_all | solution.py:95
  307.1 0.1 pad_maximum_fusion
  307.2 0.1 copy.67
  307.2 1.3 copy.60
  308.6 0.8 copy.73
  309.3 0.1 copy.74
  309.4 0.1 reshape.121
  309.5 0.8 select_reduce_fusion
  310.3 5.2 %all-to-all-done.1 = bf16[8,1,4,6144]{3,2,1,0:T(4,128)(2,1)} async-done(((bf16[8,1,4,6144]{3,2,1,0:T(4,128)(2,1)}), bf16[8,1,4,6144]{3,2,1,0:T(4,128)(2,1)}, u32[]{:S(2)}, u32[]{:S(2)}) %all-to-all-start.1) | async-done | bytes 393248 | tf_op jit(solution)/shard_map/all_to_all | solution.py:95
  315.5 1.8 reshape.89
  317.3 2.0 multiply_reduce_fusion
  319.4 0.6 fusion.22
  320.0 0.7 gather_fusion.1
  320.7 0.1 reshape.124
  320.7 0.1 broadcast_subtract_fusion
  320.8 0.1 copy.75
  320.9 0.1 copy.76
  321.0 0.6 pad_maximum_fusion.1
  (19 shorter events, 0.2 us)
Async XLA Ops:
  7.2 111.9 %copy-start = (bf16[1,256,6144]{2,1,0:T(8,128)(2,1)S(1)}, bf16[1,256,6144]{2,1,0:T(8,128)(2,1)}, u32[]{:S(2)}) copy-start(bf16[1,256,6144]{2,1,0:T(8,128)(2,1)} %param.15) | copy-start | bytes 9437188
  7.2 101.9 %all-gather.3.cloned.1.call-start = ((), (), s32[]{:S(2)}) async-start(), calls=%async_computation.3 | async-start | bytes 12976128 | tf_op jit(solution)/shard_map/all_gather | solution.py:79
  29.8 259.3 %reduce-scatter.2.cloned.1.call-start = ((), (), s32[]{:S(2)}) async-start(), calls=%async_computation.4 | async-start | bytes 12976128 | tf_op jit(solution)/shard_map/reduce_scatter | solution.py:86
  138.9 1.0 copy-start.2
  138.9 1.0 copy-start.3
  290.9 24.6 %all-to-all-start.1 = ((bf16[8,1,4,6144]{3,2,1,0:T(4,128)(2,1)}), bf16[8,1,4,6144]{3,2,1,0:T(4,128)(2,1)}, u32[]{:S(2)}, u32[]{:S(2)}) async-start(bf16[8,1,4,6144]{3,2,1,0:T(4,128)(2,1)} %bitcast.33), calls=%async_computation.2 | async-start | bytes 786432 | tf_op jit(solution)/shard_map/all_to_all | solution.py:95
  320.0 1.6 copy-start.1
Sparse Core Ops, SparseCore 0:
  29.9 79.1 all-gather.2
  139.0 149.9 reduce-scatter.1
where the time goes:
time: 329 us; the launch traced here: 328 us
  waiting for transfers between devices  191 us (58%)
  blocking collectives  53.4 us (16%)
  matrix products  35.4 us (11%)
  starting transfers between devices  16.2 us (5%)
  between operations  14.1 us (4%)
  local copies, waits for them, and re-layouts  13.9 us (4%)
  other arithmetic  4.72 us (1%)
    reduce_scatter x1, waiting for transfers between devices, on_device(): lax.psum_scatter(project(jnp.int32(0), groups * CAP * lax.axis_size('dp')...  106 us
    all_gather x1, waiting for transfers between devices, on_device(): lax.all_gather(arriving, 'dp', axis=0, tiled=True)  79.3 us
    all_gather x1, blocking collectives, in_one_piece(): filled, at, outs = (lax.all_gather(both, axis, axis=dim, tiled=True), 0, [])  36.9 us
    dot_general x1, matrix products, project(): return jnp.dot(block, w_down[local], preferred_element_type=jnp.float32)  19.8 us
    all_to_all x1, blocking collectives, on_device(): lax.all_to_all(dispatched, 'expert', split_axis=0, concat_axis=0, tiled=T...  16.5 us
    all_to_all x1, starting transfers between devices, on_device(): lax.all_to_all(stacked.astype(jnp.bfloat16), 'expert', split_axis=0, conc...  16.1 us
    dot_general x1, matrix products, activate(): gate = jnp.dot(piece, w_gate[local], preferred_element_type=jnp.float32)  9.95 us
  transfers between devices with their start and end apart: 3, of which 3 were waited for; matrix products, arithmetic and copies ran while one was open for 3% of the time, Pallas kernels for 0%

commit v1 on v0

--- a/solution.py
+++ b/solution.py
@@ -76,7 +76,14 @@
         upward = jnp.dot(piece, w_up[local], preferred_element_type=jnp.float32)
         return (jax.nn.silu(gate) * upward).astype(jnp.bfloat16)
 
-    hidden_list.append(activate(lax.all_gather(arriving, "dp", axis=0, tiled=True), jnp.int32(0)))
+    hidden_list.append(
+        activate(
+            jnp.concatenate(
+                lax.all_to_all(jnp.stack([arriving] * lax.axis_size("dp")), "dp", 0, 0), axis=0
+            ),
+            jnp.int32(0),
+        )
+    )
     local = 0
 
     def project(start, count, local=local):

time: 329 us -> 531 us (1.61)
  blocking collectives: 53.4 us -> 340 us
  waiting for transfers between devices: 191 us -> 106 us
  local copies, waits for them, and re-layouts: 13.9 us -> 24.8 us
  starting transfers between devices: 16.2 us -> 7.57 us
  matrix products: 35.4 us -> 29.9 us
    all_to_all x0 -> x1, blocking collectives: none -> 285 us  [on_device(): lax.all_to_all(jnp.stack([arriving] * lax.axis_size('dp')), 'dp', 0, 0)]
    all_gather x1 -> x0, waiting for transfers between devices: 79.3 us -> none  [on_device(): lax.all_gather(arriving, 'dp', axis=0, tiled=True)]
    all_to_all x1, starting transfers between devices: 16.1 us -> 7.53 us  [on_device(): lax.all_to_all(stacked.astype(jnp.bfloat16), 'expert', split_axis=0, conc...]
    reduce_scatter x1, waiting for transfers between devices: 106 us -> 99.2 us  [on_device(): lax.psum_scatter(project(jnp.int32(0), groups * CAP * lax.axis_size('dp')...]
    another operation x1 -> x2, local copies, waits for them, and re-layouts: 0.83 us -> 7.22 us  [on_device(): jnp.stack([arriving] * lax.axis_size('dp'))]
    dot_general x1, matrix products: 9.95 us -> 4.48 us  [activate(): gate = jnp.dot(piece, w_gate[local], preferred_element_type=jnp.float32)]
  transfers between devices with their start and end apart: 3 -> 2, of which waited for: 3 -> 2; matrix products, arithmetic and copies ran while one was open for 3% -> 2% of each run, Pallas kernels for 0% -> 0%
where the time goes in v1:
time: 531 us; the launch traced here: 528 us
  blocking collectives  340 us (64%)
  waiting for transfers between devices  106 us (20%)
  matrix products  29.9 us (6%)
  local copies, waits for them, and re-layouts  24.8 us (5%)
  between operations  14.1 us (3%)
  starting transfers between devices  7.57 us (1%)
    all_to_all x1, blocking collectives, on_device(): lax.all_to_all(jnp.stack([arriving] * lax.axis_size('dp')), 'dp', 0, 0)  285 us
    reduce_scatter x1, waiting for transfers between devices, on_device(): lax.psum_scatter(project(jnp.int32(0), groups * CAP * lax.axis_size('dp')...  99.2 us
    all_gather x1, blocking collectives, in_one_piece(): filled, at, outs = (lax.all_gather(both, axis, axis=dim, tiled=True), 0, [])  38.6 us
    dot_general x1, matrix products, project(): return jnp.dot(block, w_down[local], preferred_element_type=jnp.float32)  19.8 us
    all_to_all x1, blocking collectives, on_device(): lax.all_to_all(dispatched, 'expert', split_axis=0, concat_axis=0, tiled=T...  16.6 us
  transfers between devices with their start and end apart: 2, of which 2 were waited for; matrix products, arithmetic and copies ran while one was open for 2% of the time, Pallas kernels for 0%

profile of v1, /device:TPU:2, one launch (start us, length us, event | category | flops | bytes accessed | tf_op | source)
XLA Modules:
  0.0 527.5 jit_solution(17736521716468296167)
XLA Ops:
  7.2 0.9 copy.58
  8.1 0.1 eq.48
  8.2 0.1 fusion.30
  8.3 0.2 select_reduce_fusion.1
  8.5 0.5 and_select_fusion.2
  9.0 1.1 fusion.21
  10.1 1.5 convolution_convert_fusion.1
  11.6 0.9 reshape.93
  12.4 16.6 %all_to_all.15 = bf16[8,1,4,6144]{3,2,1,0:T(4,128)(2,1)} all-to-all(bf16[8,1,4,6144]{3,2,1,0:T(4,128)(2,1)} %bitcast.37), channel_id=1, replica_groups=mesh['dp'=32,'expert'=8] {'expert'}, dimensions={0} | all-to-all | bytes 786432 | tf_op jit(solution)/shard_map/all_to_all | solution.py:63
  29.0 1.1 stack_reshape_squeeze.2
  30.1 6.1 %stack.14 = bf16[32,32,6144]{2,1,0:T(8,128)(2,1)} broadcast(bf16[32,6144]{1,0:T(8,128)(2,1)S(1)} %stack_reshape_squeeze.2), dimensions={1,2} | broadcast | bytes 12976128 | tf_op jit(solution)/shard_map/stack | solution.py:82
  36.3 285.0 %all_to_all.16 = bf16[32,32,6144]{2,1,0:T(8,128)(2,1)S(1)} all-to-all(bf16[32,32,6144]{2,1,0:T(8,128)(2,1)} %stack.14), channel_id=1, replica_groups=mesh['dp'=32,'expert'=8] {'dp'}, dimensions={0} | all-to-all | bytes 25165824 | tf_op jit(solution)/shard_map/all_to_all | solution.py:82
  321.3 4.5 copy-done.2
  325.7 4.5 fusion.3
  330.2 19.8 %convolution_convert_fusion = bf16[1024,6144]{1,0:T(8,128)(2,1)} fusion(bf16[1,256,6144]{2,1,0:T(8,128)(2,1)S(1)} %copy-done, bf16[1024,6144]{1,0:T(8,128)(2,1)} %bitcast.35, bf16[1,6144,256]{2,1,0:T(8,128)(2,1)} %param.14, f32[1024,256]{1,0:T(8,128)} %fusion.3), kind=kOutput, calls=%fused_computation.2 | convolution fusion | flops 6450315264 | bytes 32505856 | tf_op jit(solution)/shard_map/dot_general | solution.py:91
  350.1 0.1 reduce_sum.39
  350.2 0.6 multiply_add_fusion
  350.8 0.1 copy.65
  350.8 0.1 copy.66
  350.9 0.1 reshape.122
  351.0 38.6 %all-gather = f32[32,192,16]{1,2,0:T(8,128)S(1)} all-gather(f32[1,192,16]{1,2,0:T(8,128)S(1)} %maximum_bitcast_fusion), channel_id=1, replica_groups=mesh['dp'=32,'expert'=8] {'dp'}, dimensions={0}, use_global_device_ids=true | all-gather | bytes 405504 | tf_op jit(solution)/shard_map/all_gather | solution.py:12
  389.7 1.1 copy.64
  390.8 1.3 reshape.120
  392.0 1.5 fusion.20
  393.5 0.7 gather_fusion
  394.2 0.1 reshape.125
  394.3 0.8 copy.70
  395.0 0.6 clamp_shift-left_fusion
  395.6 0.1 broadcast_subtract_fusion.1
  395.7 99.2 %reduce-scatter.2.cloned.1.call-done = bf16[32,6144]{1,0:T(8,128)(2,1)} async-done(((bf16[1024,6144]{1,0:T(8,128)(2,1)}), bf16[32,6144]{1,0:T(8,128)(2,1)}) %reduce-scatter.2.cloned.1.call-update) | async-done | bytes 393232 | tf_op jit(solution)/shard_map/reduce_scatter | solution.py:93
  494.9 1.9 convert_element_type.47
  496.8 7.5 %all-to-all-start.2 = ((bf16[8,1,4,6144]{3,2,1,0:T(4,128)(2,1)}), bf16[8,1,4,6144]{3,2,1,0:T(4,128)(2,1)}, u32[]{:S(2)}, u32[]{:S(2)}) async-start(bf16[8,1,4,6144]{3,2,1,0:T(4,128)(2,1)} %bitcast.36), calls=%async_computation.3 | async-start | bytes 786432 | tf_op jit(solution)/shard_map/all_to_all | solution.py:102
  504.4 0.1 copy.67
  504.5 1.3 copy.60
  505.8 0.8 copy.73
  506.6 0.1 copy.74
  506.7 0.1 reshape.127
  506.7 0.8 select_reduce_fusion
  507.5 7.1 %all-to-all-done.2 = bf16[8,1,4,6144]{3,2,1,0:T(4,128)(2,1)} async-done(((bf16[8,1,4,6144]{3,2,1,0:T(4,128)(2,1)}), bf16[8,1,4,6144]{3,2,1,0:T(4,128)(2,1)}, u32[]{:S(2)}, u32[]{:S(2)}) %all-to-all-start.2) | async-done | bytes 393248 | tf_op jit(solution)/shard_map/all_to_all | solution.py:102
  514.6 1.8 reshape.95
  516.5 2.0 multiply_reduce_fusion
  518.5 0.6 fusion.22
  519.1 0.7 gather_fusion.1
  519.8 0.1 reshape.130
  519.8 0.1 broadcast_subtract_fusion
  519.9 0.1 copy.75
  520.0 0.1 copy.76
  520.1 0.6 pad_maximum_fusion.1
  (22 shorter events, 0.2 us)
Async XLA Ops:
  7.2 323.0 %copy-start = (bf16[1,256,6144]{2,1,0:T(8,128)(2,1)S(1)}, bf16[1,256,6144]{2,1,0:T(8,128)(2,1)}, u32[]{:S(2)}) copy-start(bf16[1,256,6144]{2,1,0:T(8,128)(2,1)} %param.15) | copy-start | bytes 9437188
  7.2 487.7 %reduce-scatter.2.cloned.1.call-start = ((), (), s32[]{:S(2)}) async-start(), calls=%async_computation.4 | async-start | bytes 12976128 | tf_op jit(solution)/shard_map/reduce_scatter | solution.py:93
  36.3 289.5 %copy-start.5 = (bf16[1,6144,256]{2,1,0:T(8,128)(2,1)S(1)}, bf16[1,6144,256]{2,1,0:T(8,128)(2,1)}, u32[]{:S(2)}) copy-start(bf16[1,6144,256]{2,1,0:T(8,128)(2,1)} %param.13) | copy-start | bytes 9437188
  321.3 4.5 copy-start.2
  350.0 1.0 copy-start.3
  350.0 1.0 copy-start.4
  496.8 17.8 %all-to-all-start.2 = ((bf16[8,1,4,6144]{3,2,1,0:T(4,128)(2,1)}), bf16[8,1,4,6144]{3,2,1,0:T(4,128)(2,1)}, u32[]{:S(2)}, u32[]{:S(2)}) async-start(bf16[8,1,4,6144]{3,2,1,0:T(4,128)(2,1)} %bitcast.36), calls=%async_computation.3 | async-start | bytes 786432 | tf_op jit(solution)/shard_map/all_to_all | solution.py:102
  519.1 1.6 copy-start.1
Sparse Core Ops, SparseCore 0:
  350.2 144.6 reduce-scatter.1
